TPU v7x, 32 devices: a whole 2x2x4 slice. The times are simulated.
32 devices in a mesh: dp: 4 (over x, core), pp: 8 (over z, y).
Axes of the slice: x: 2, y: 2, z: 4, core: 2. Of those that a mesh axis runs over, the one named last changes fastest.
Arguments:
- hidden: bfloat16 [512, 4096], P(('dp', 'pp')), may hold values from -400 to 400
- norm_gain: float32 [4096], replicated, may hold values from 0.1 to 1.9
- head: bfloat16 [32768, 4096], P(('dp', 'pp')), may hold values from -32 to 32
- targets: int32 [512], P(('dp', 'pp')), may hold values from 0 to 32767
- route: int32 [32], replicated, may hold values from 0 to 3
Outputs:
- token_loss: float32 [512], P(('dp', 'pp'))
- pipe_loss: float32 [4], replicated
All inputs are finite; a program needn't handle non-finite values.
Results may differ from a plain program's by a relative error of at most 0.00053.
Values may be sent and summed in bfloat16 or wider, within the bound.
A program may use at most 64 MiB of HBM per device.

v0:
```python
import math
import jax
import jax.numpy as jnp
from jax import lax
from jax.sharding import PartitionSpec as P


def rms_normal(rows, gain):
    wide = rows.astype(jnp.float32)
    factor = lax.rsqrt(jnp.mean(wide * wide, axis=1, keepdims=True) + 1e-05)
    return (wide * factor * gain).astype(jnp.bfloat16)


def tile_stats(normed, labels, head, first):
    total = normed.shape[0]
    block = math.gcd(total, 512)
    columns = first + lax.iota(jnp.int32, head.shape[0])

    def one_block(pair):
        rows, marks = pair
        logits = lax.dot_general(
            rows, head, (((1,), (1,)), ((), ())), preferred_element_type=jnp.float32
        )
        peak = jnp.max(logits, axis=1)
        mass = jnp.sum(jnp.exp(logits - peak[:, None]), axis=1)
        hit = jnp.sum(jnp.where(marks[:, None] == columns[None, :], logits, 0.0), axis=1)
        return (peak, mass, hit)

    peak, mass, hit = lax.map(
        one_block,
        (
            normed.reshape(total // block, block, normed.shape[1]),
            labels.reshape(total // block, block),
        ),
    )
    return (peak.reshape(total), mass.reshape(total), hit.reshape(total))


def shards(hidden, norm_gain, head, targets, route):
    place = lax.axis_index(("dp", "pp"))
    devices = lax.axis_size(("dp", "pp"))
    pipes = lax.axis_size("dp")
    rows = hidden.shape[0]
    gathered, labels = (
        lax.all_gather(hidden, ("dp", "pp"), axis=0, tiled=True),
        lax.all_gather(targets, ("dp", "pp"), axis=0, tiled=True),
    )
    normed = rms_normal(gathered, norm_gain)
    peak, mass, hit = tile_stats(normed, labels, head, place * head.shape[0])
    peak_all, mass_all, hit_all = (
        lax.all_to_all(
            peak.reshape(devices, rows), ("dp", "pp"), split_axis=0, concat_axis=0, tiled=True
        ),
        lax.all_to_all(
            mass.reshape(devices, rows), ("dp", "pp"), split_axis=0, concat_axis=0, tiled=True
        ),
        lax.all_to_all(
            hit.reshape(devices, rows), ("dp", "pp"), split_axis=0, concat_axis=0, tiled=True
        ),
    )
    top = jnp.max(peak_all, axis=0)
    mass_own = jnp.sum(mass_all * jnp.exp(peak_all - top[None, :]), axis=0)
    hit_own = jnp.sum(hit_all, axis=0)
    token_loss = top + jnp.log(mass_own) - hit_own
    mine = route[place]
    credit = jnp.where(lax.iota(jnp.int32, pipes) == mine, jnp.sum(token_loss), 0.0)
    summed = lax.psum(credit, ("dp", "pp"))
    pipe_loss = summed / (rows * devices // pipes)
    return (token_loss, pipe_loss)


def solution(mesh):
    placed = (P(("dp", "pp"), None), P(), P(("dp", "pp"), None), P(("dp", "pp")), P())
    return jax.shard_map(
        shards, mesh=mesh, in_specs=placed, out_specs=(P(("dp", "pp")), P()), check_vma=False
    )
```

profile of v0, /device:TPU:0, one launch (start us, length us, event | category | flops | bytes accessed | tf_op | source)
XLA Modules:
  0.0 165.2 jit_solution(11259137968374212607)
XLA Ops:
  7.2 0.0 copy-start.1
  7.2 0.0 all-gather.2.cloned.1.call-start
  7.2 0.7 all-gather.2.cloned.1.call-update
  7.9 0.9 dynamic-update-slice
  8.8 42.0 %all-reduce = s32[512]{0:T(512)S(1)} all-reduce(s32[512]{0:T(512)S(1)} %dynamic-update-slice), channel_id=1, replica_groups=mesh['dp'=4,'pp'=8] {'dp','pp'}, use_global_device_ids=true, to_apply=%add | all-reduce | flops 512 | bytes 4096
  50.8 24.9 %all-gather.2.cloned.1.call-done = bf16[512,4096]{1,0:T(8,128)(2,1)} async-done(((bf16[16,4096]{1,0:T(8,128)(2,1)}), bf16[512,4096]{1,0:T(8,128)(2,1)}) %all-gather.2.cloned.1.call-update) | async-done | bytes 4194320 | tf_op jit(solution)/shard_map/all_gather | solution.py:45
  75.7 0.0 copy-start
  75.7 3.2 %fusion = f32[512]{0:T(512)S(1)} fusion(bf16[512,4096]{1,0:T(8,128)(2,1)} %all-gather.2.cloned.1.call-done), kind=kLoop, calls=%fused_computation.2 | loop fusion | flops 6290944 | bytes 4196352 | tf_op jit(solution)/shard_map/reduce_sum | solution.py:10
  79.0 0.0 copy-done.1
  79.0 0.2 copy-done
  79.2 0.0 copy-start.2
  79.2 7.4 %fusion.8 = (f32[512]{0:T(512)S(1)}, f32[512,1024]{1,0:T(8,128)S(1)}) fusion(bf16[1024,4096]{1,0:T(8,128)(2,1)} %param.7, bf16[512,4096]{1,0:T(8,128)(2,1)S(1)} %copy-done, f32[4096]{0:T(1024)S(1)} %copy-done.1, f32[512]{0:T(512)S(1)} %add_rsqrt_fusion), kind=kOutput, calls=%fused_computation.17 | convolution fusion | flops 4303879680 | bytes 14700544 | tf_op jit(solution)/shard_map/while/body/eval_jaxpr/dot_general | solution.py:21
  86.6 0.7 all_to_all.22
  87.3 3.4 %all-to-all-start = ((f32[32,1,16]{2,1,0:T(1,128)}), f32[32,1,16]{2,1,0:T(1,128)S(1)}, u32[]{:S(2)}, u32[]{:S(2)}) async-start(f32[32,1,16]{2,1,0:T(1,128)} %bitcast), calls=%async_computation | async-start | bytes 32768 | tf_op jit(solution)/shard_map/all_to_all | solution.py:51
  90.7 0.6 exponential_reduce_fusion
  91.3 0.7 all_to_all.24
  92.0 5.8 %all-to-all-done = f32[32,1,16]{2,1,0:T(1,128)S(1)} async-done(((f32[32,1,16]{2,1,0:T(1,128)}), f32[32,1,16]{2,1,0:T(1,128)S(1)}, u32[]{:S(2)}, u32[]{:S(2)}) %all-to-all-start) | async-done | bytes 2080 | tf_op jit(solution)/shard_map/all_to_all | solution.py:51
  97.9 2.6 %all-to-all-start.1 = ((f32[32,1,16]{2,1,0:T(1,128)}), f32[32,1,16]{2,1,0:T(1,128)S(1)}, u32[]{:S(2)}, u32[]{:S(2)}) async-start(f32[32,1,16]{2,1,0:T(1,128)} %bitcast.1), calls=%async_computation.1 | async-start | bytes 32768 | tf_op jit(solution)/shard_map/all_to_all | solution.py:54
  100.4 0.0 copy-done.2
  100.4 0.6 dynamic_slice.9
  101.1 0.7 all_to_all.28
  101.7 0.1 reduce_max.20
  101.8 5.8 %all-to-all-done.1 = f32[32,1,16]{2,1,0:T(1,128)S(1)} async-done(((f32[32,1,16]{2,1,0:T(1,128)}), f32[32,1,16]{2,1,0:T(1,128)S(1)}, u32[]{:S(2)}, u32[]{:S(2)}) %all-to-all-start.1) | async-done | bytes 2080 | tf_op jit(solution)/shard_map/all_to_all | solution.py:54
  107.6 2.5 %all-to-all-start.2 = ((f32[32,1,16]{2,1,0:T(1,128)}), f32[32,1,16]{2,1,0:T(1,128)S(1)}, u32[]{:S(2)}, u32[]{:S(2)}) async-start(f32[32,1,16]{2,1,0:T(1,128)} %bitcast.4), calls=%async_computation.2 | async-start | bytes 32768 | tf_op jit(solution)/shard_map/all_to_all | solution.py:57
  110.1 7.1 %all-to-all-done.2 = f32[32,1,16]{2,1,0:T(1,128)S(1)} async-done(((f32[32,1,16]{2,1,0:T(1,128)}), f32[32,1,16]{2,1,0:T(1,128)S(1)}, u32[]{:S(2)}, u32[]{:S(2)}) %all-to-all-start.2) | async-done | bytes 2080 | tf_op jit(solution)/shard_map/all_to_all | solution.py:57
  117.2 0.1 reduce_sum.60
  117.3 1.1 fusion.7
  118.4 1.3 compare_select_fusion
  119.7 38.2 %psum.7 = f32[4]{0:T(128)S(1)} all-reduce(f32[4]{0:T(128)S(1)} %compare_select_fusion), channel_id=1, replica_groups=mesh['dp'=4,'pp'=8] {'dp','pp'}, use_global_device_ids=true, to_apply=%region_8.9 | all-reduce | flops 4 | bytes 32 | tf_op jit(solution)/shard_map/psum | solution.py:67
  157.9 0.5 broadcast_multiply_fusion
  (4 shorter events, 0.0 us)
Async XLA Ops:
  7.2 71.8 %copy-start.1 = (f32[4096]{0:T(1024)S(1)}, f32[4096]{0:T(1024)}, u32[]{:S(2)}) copy-start(f32[4096]{0:T(1024)} %param.6) | copy-start | bytes 49156
  7.2 68.6 %all-gather.2.cloned.1.call-start = ((), (), s32[]{:S(2)}) async-start(), calls=%async_computation.3 | async-start | bytes 4325376 | tf_op jit(solution)/shard_map/all_gather | solution.py:45
  75.7 3.4 %copy-start = (bf16[512,4096]{1,0:T(8,128)(2,1)S(1)}, bf16[512,4096]{1,0:T(8,128)(2,1)}, u32[]{:S(2)}) copy-start(bf16[512,4096]{1,0:T(8,128)(2,1)} %all-gather.2.cloned.1.call-done) | copy-start | bytes 12582916
  79.2 21.2 %copy-start.2 = (s32[32]{0:T(128)S(1)}, s32[32]{0:T(128)}, u32[]{:S(2)}) copy-start(s32[32]{0:T(128)} %param.9) | copy-start | bytes 388
  87.3 10.5 %all-to-all-start = ((f32[32,1,16]{2,1,0:T(1,128)}), f32[32,1,16]{2,1,0:T(1,128)S(1)}, u32[]{:S(2)}, u32[]{:S(2)}) async-start(f32[32,1,16]{2,1,0:T(1,128)} %bitcast), calls=%async_computation | async-start | bytes 32768 | tf_op jit(solution)/shard_map/all_to_all | solution.py:51
  97.9 9.7 %all-to-all-start.1 = ((f32[32,1,16]{2,1,0:T(1,128)}), f32[32,1,16]{2,1,0:T(1,128)S(1)}, u32[]{:S(2)}, u32[]{:S(2)}) async-start(f32[32,1,16]{2,1,0:T(1,128)} %bitcast.1), calls=%async_computation.1 | async-start | bytes 32768 | tf_op jit(solution)/shard_map/all_to_all | solution.py:54
  107.6 9.6 %all-to-all-start.2 = ((f32[32,1,16]{2,1,0:T(1,128)}), f32[32,1,16]{2,1,0:T(1,128)S(1)}, u32[]{:S(2)}, u32[]{:S(2)}) async-start(f32[32,1,16]{2,1,0:T(1,128)} %bitcast.4), calls=%async_computation.2 | async-start | bytes 32768 | tf_op jit(solution)/shard_map/all_to_all | solution.py:57
Sparse Core Ops, SparseCore 0:
  11.1 64.6 all-gather.1
where the time goes:
time: 166 us; the launch traced here: 165 us
  blocking collectives  80.3 us (48%)
  waiting for transfers between devices  44.3 us (27%)
  between operations  14.1 us (8%)
  starting transfers between devices  8.47 us (5%)
  matrix products  7.43 us (4%)
  other arithmetic  6.91 us (4%)
  local copies, waits for them, and re-layouts  3.72 us (2%)
    unnamed x1, blocking collectives  42 us
    psum x1, blocking collectives, shards(): summed = lax.psum(credit, ('dp', 'pp'))  38.2 us
    all_gather x1, waiting for transfers between devices, shards(): lax.all_gather(hidden, ('dp', 'pp'), axis=0, tiled=True)  24.9 us
    dot_general x1, matrix products, one_block(): lax.dot_general(rows, head, (((1,), (1,)), ((), ())), preferred_element_t...  7.43 us
    all_to_all x1, waiting for transfers between devices, shards(): lax.all_to_all(hit.reshape(devices, rows), ('dp', 'pp'), split_axis=0, co...  7.12 us
    all_to_all x1, waiting for transfers between devices, shards(): lax.all_to_all(peak.reshape(devices, rows), ('dp', 'pp'), split_axis=0, c...  5.84 us
    all_to_all x1, waiting for transfers between devices, shards(): lax.all_to_all(mass.reshape(devices, rows), ('dp', 'pp'), split_axis=0, c...  5.78 us
    all_to_all x1, starting transfers between devices, shards(): lax.all_to_all(peak.reshape(devices, rows), ('dp', 'pp'), split_axis=0, c...  3.39 us
  transfers between devices with their start and end apart: 4, of which 4 were waited for; matrix products, arithmetic and copies ran while one was open for 1% of the time, Pallas kernels for 0%

commit v1 on v0

--- a/solution.py
+++ b/solution.py
@@ -64,7 +64,8 @@
     token_loss = top + jnp.log(mass_own) - hit_own
     mine = route[place]
     credit = jnp.where(lax.iota(jnp.int32, pipes) == mine, jnp.sum(token_loss), 0.0)
-    summed = lax.psum(credit, ("dp", "pp"))
+    parts = lax.all_gather(credit, ("dp", "pp"), axis=0, tiled=False)
+    summed = parts.sum(axis=0)
     pipe_loss = summed / (rows * devices // pipes)
     return (token_loss, pipe_loss)
 

time: 166 us -> 191 us (1.15)
  blocking collectives: 80.3 us -> 106 us
    all_gather x0 -> x1, blocking collectives: none -> 64 us  [shards(): parts = lax.all_gather(credit, ('dp', 'pp'), axis=0, tiled=False)]
    psum x1 -> x0, blocking collectives: 38.2 us -> none  [shards(): summed = lax.psum(credit, ('dp', 'pp'))]
where the time goes in v1:
time: 191 us
  blocking collectives  106 us (55%)
  waiting for transfers between devices  44.3 us (23%)
  between operations  14.1 us (7%)
  starting transfers between devices  8.47 us (4%)
  matrix products  7.43 us (4%)
  other arithmetic  6.96 us (4%)
  local copies, waits for them, and re-layouts  3.72 us (2%)
    all_gather x1, blocking collectives, shards(): parts = lax.all_gather(credit, ('dp', 'pp'), axis=0, tiled=False)  64 us
    unnamed x1, blocking collectives  42 us
    all_gather x1, waiting for transfers between devices, shards(): lax.all_gather(hidden, ('dp', 'pp'), axis=0, tiled=True)  24.9 us
    dot_general x1, matrix products, one_block(): lax.dot_general(rows, head, (((1,), (1,)), ((), ())), preferred_element_t...  7.43 us
    all_to_all x1, waiting for transfers between devices, shards(): lax.all_to_all(hit.reshape(devices, rows), ('dp', 'pp'), split_axis=0, co...  7.12 us
    all_to_all x1, waiting for transfers between devices, shards(): lax.all_to_all(peak.reshape(devices, rows), ('dp', 'pp'), split_axis=0, c...  5.84 us
    all_to_all x1, waiting for transfers between devices, shards(): lax.all_to_all(mass.reshape(devices, rows), ('dp', 'pp'), split_axis=0, c...  5.78 us
  transfers between devices with their start and end apart: 4, of which 4 were waited for; matrix products, arithmetic and copies ran while one was open for 1% of the time, Pallas kernels for 0%

profile of v1, /device:TPU:0, one launch (start us, length us, event | category | flops | bytes accessed | tf_op | source)
XLA Modules:
  0.0 191.1 jit_solution(15503443843219503389)
XLA Ops:
  7.2 0.0 copy-start.1
  7.2 0.0 all-gather.3.cloned.1.call-start
  7.2 0.7 all-gather.3.cloned.1.call-update
  7.9 0.9 dynamic-update-slice
  8.8 42.0 %all-reduce = s32[512]{0:T(512)S(1)} all-reduce(s32[512]{0:T(512)S(1)} %dynamic-update-slice), channel_id=1, replica_groups=mesh['dp'=4,'pp'=8] {'dp','pp'}, use_global_device_ids=true, to_apply=%add | all-reduce | flops 512 | bytes 4096
  50.8 24.9 %all-gather.3.cloned.1.call-done = bf16[512,4096]{1,0:T(8,128)(2,1)} async-done(((bf16[16,4096]{1,0:T(8,128)(2,1)}), bf16[512,4096]{1,0:T(8,128)(2,1)}) %all-gather.3.cloned.1.call-update) | async-done | bytes 4194320 | tf_op jit(solution)/shard_map/all_gather | solution.py:45
  75.7 0.0 copy-start
  75.7 3.2 %fusion = f32[512]{0:T(512)S(1)} fusion(bf16[512,4096]{1,0:T(8,128)(2,1)} %all-gather.3.cloned.1.call-done), kind=kLoop, calls=%fused_computation.2 | loop fusion | flops 6290944 | bytes 4196352 | tf_op jit(solution)/shard_map/reduce_sum | solution.py:10
  79.0 0.0 copy-done.1
  79.0 0.2 copy-done
  79.2 0.0 copy-start.2
  79.2 7.4 %fusion.9 = (f32[512]{0:T(512)S(1)}, f32[512,1024]{1,0:T(8,128)S(1)}) fusion(bf16[1024,4096]{1,0:T(8,128)(2,1)} %param.7, bf16[512,4096]{1,0:T(8,128)(2,1)S(1)} %copy-done, f32[4096]{0:T(1024)S(1)} %copy-done.1, f32[512]{0:T(512)S(1)} %add_rsqrt_fusion), kind=kOutput, calls=%fused_computation.18 | convolution fusion | flops 4303879680 | bytes 14700544 | tf_op jit(solution)/shard_map/while/body/eval_jaxpr/dot_general | solution.py:21
  86.6 0.7 all_to_all.22
  87.3 3.4 %all-to-all-start = ((f32[32,1,16]{2,1,0:T(1,128)}), f32[32,1,16]{2,1,0:T(1,128)S(1)}, u32[]{:S(2)}, u32[]{:S(2)}) async-start(f32[32,1,16]{2,1,0:T(1,128)} %bitcast), calls=%async_computation | async-start | bytes 32768 | tf_op jit(solution)/shard_map/all_to_all | solution.py:51
  90.7 0.6 exponential_reduce_fusion
  91.3 0.7 all_to_all.24
  92.0 5.8 %all-to-all-done = f32[32,1,16]{2,1,0:T(1,128)S(1)} async-done(((f32[32,1,16]{2,1,0:T(1,128)}), f32[32,1,16]{2,1,0:T(1,128)S(1)}, u32[]{:S(2)}, u32[]{:S(2)}) %all-to-all-start) | async-done | bytes 2080 | tf_op jit(solution)/shard_map/all_to_all | solution.py:51
  97.9 2.6 %all-to-all-start.1 = ((f32[32,1,16]{2,1,0:T(1,128)}), f32[32,1,16]{2,1,0:T(1,128)S(1)}, u32[]{:S(2)}, u32[]{:S(2)}) async-start(f32[32,1,16]{2,1,0:T(1,128)} %bitcast.1), calls=%async_computation.1 | async-start | bytes 32768 | tf_op jit(solution)/shard_map/all_to_all | solution.py:54
  100.4 0.0 copy-done.2
  100.4 0.6 dynamic_slice.9
  101.1 0.7 all_to_all.28
  101.7 0.1 reduce_max.20
  101.8 5.8 %all-to-all-done.1 = f32[32,1,16]{2,1,0:T(1,128)S(1)} async-done(((f32[32,1,16]{2,1,0:T(1,128)}), f32[32,1,16]{2,1,0:T(1,128)S(1)}, u32[]{:S(2)}, u32[]{:S(2)}) %all-to-all-start.1) | async-done | bytes 2080 | tf_op jit(solution)/shard_map/all_to_all | solution.py:54
  107.6 2.5 %all-to-all-start.2 = ((f32[32,1,16]{2,1,0:T(1,128)}), f32[32,1,16]{2,1,0:T(1,128)S(1)}, u32[]{:S(2)}, u32[]{:S(2)}) async-start(f32[32,1,16]{2,1,0:T(1,128)} %bitcast.4), calls=%async_computation.2 | async-start | bytes 32768 | tf_op jit(solution)/shard_map/all_to_all | solution.py:57
  110.1 7.1 %all-to-all-done.2 = f32[32,1,16]{2,1,0:T(1,128)S(1)} async-done(((f32[32,1,16]{2,1,0:T(1,128)}), f32[32,1,16]{2,1,0:T(1,128)S(1)}, u32[]{:S(2)}, u32[]{:S(2)}) %all-to-all-start.2) | async-done | bytes 2080 | tf_op jit(solution)/shard_map/all_to_all | solution.py:57
  117.2 0.1 reduce_sum.69
  117.3 1.1 fusion.8
  118.4 1.3 fusion.7
  119.7 64.0 %all-gather = f32[32,1,4]{2,1,0:T(1,128)S(1)} all-gather(f32[1,1,4]{2,1,0:T(1,128)S(1)} %fusion.7), channel_id=1, replica_groups=mesh['dp'=4,'pp'=8] {'dp','pp'}, dimensions={0}, use_global_device_ids=true | all-gather | bytes 528 | tf_op jit(solution)/shard_map/all_gather | solution.py:67
  183.6 0.1 reduce_sum.71
  183.7 0.5 broadcast_multiply_fusion
  (4 shorter events, 0.0 us)
Async XLA Ops:
  7.2 71.8 %copy-start.1 = (f32[4096]{0:T(1024)S(1)}, f32[4096]{0:T(1024)}, u32[]{:S(2)}) copy-start(f32[4096]{0:T(1024)} %param.6) | copy-start | bytes 49156
  7.2 68.6 %all-gather.3.cloned.1.call-start = ((), (), s32[]{:S(2)}) async-start(), calls=%async_computation.3 | async-start | bytes 4325376 | tf_op jit(solution)/shard_map/all_gather | solution.py:45
  75.7 3.4 %copy-start = (bf16[512,4096]{1,0:T(8,128)(2,1)S(1)}, bf16[512,4096]{1,0:T(8,128)(2,1)}, u32[]{:S(2)}) copy-start(bf16[512,4096]{1,0:T(8,128)(2,1)} %all-gather.3.cloned.1.call-done) | copy-start | bytes 12582916
  79.2 21.2 %copy-start.2 = (s32[32]{0:T(128)S(1)}, s32[32]{0:T(128)}, u32[]{:S(2)}) copy-start(s32[32]{0:T(128)} %param.9) | copy-start | bytes 388
  87.3 10.5 %all-to-all-start = ((f32[32,1,16]{2,1,0:T(1,128)}), f32[32,1,16]{2,1,0:T(1,128)S(1)}, u32[]{:S(2)}, u32[]{:S(2)}) async-start(f32[32,1,16]{2,1,0:T(1,128)} %bitcast), calls=%async_computation | async-start | bytes 32768 | tf_op jit(solution)/shard_map/all_to_all | solution.py:51
  97.9 9.7 %all-to-all-start.1 = ((f32[32,1,16]{2,1,0:T(1,128)}), f32[32,1,16]{2,1,0:T(1,128)S(1)}, u32[]{:S(2)}, u32[]{:S(2)}) async-start(f32[32,1,16]{2,1,0:T(1,128)} %bitcast.1), calls=%async_computation.1 | async-start | bytes 32768 | tf_op jit(solution)/shard_map/all_to_all | solution.py:54
  107.6 9.6 %all-to-all-start.2 = ((f32[32,1,16]{2,1,0:T(1,128)}), f32[32,1,16]{2,1,0:T(1,128)S(1)}, u32[]{:S(2)}, u32[]{:S(2)}) async-start(f32[32,1,16]{2,1,0:T(1,128)} %bitcast.4), calls=%async_computation.2 | async-start | bytes 32768 | tf_op jit(solution)/shard_map/all_to_all | solution.py:57
Sparse Core Ops, SparseCore 0:
  11.1 64.6 all-gather.2

commit v2 on v0

--- a/solution.py
+++ b/solution.py
@@ -64,7 +64,8 @@
     token_loss = top + jnp.log(mass_own) - hit_own
     mine = route[place]
     credit = jnp.where(lax.iota(jnp.int32, pipes) == mine, jnp.sum(token_loss), 0.0)
-    summed = lax.psum(credit, ("dp", "pp"))
+    panels_drive = lambda view: lax.psum(lax.psum(view, axis_name="pp"), axis_name="dp")
+    summed = panels_drive(credit)
     pipe_loss = summed / (rows * devices // pipes)
     return (token_loss, pipe_loss)
 

time: 166 us -> 151 us (0.910)
  blocking collectives: 80.3 us -> 65.8 us
    psum x1 -> x2, blocking collectives: 38.2 us -> 23.7 us  [the longest x1 17.7 us: shards(): lax.psum(view, axis_name='pp')]
where the time goes in v2:
time: 151 us
  blocking collectives  65.8 us (44%)
  waiting for transfers between devices  44.3 us (29%)
  between operations  14.1 us (9%)
  starting transfers between devices  8.47 us (6%)
  matrix products  7.43 us (5%)
  other arithmetic  6.91 us (5%)
  local copies, waits for them, and re-layouts  3.72 us (2%)
    unnamed x1, blocking collectives  42 us
    all_gather x1, waiting for transfers between devices, shards(): lax.all_gather(hidden, ('dp', 'pp'), axis=0, tiled=True)  24.9 us
    psum x1, blocking collectives, shards(): lax.psum(view, axis_name='pp')  17.7 us
    dot_general x1, matrix products, one_block(): lax.dot_general(rows, head, (((1,), (1,)), ((), ())), preferred_element_t...  7.43 us
    all_to_all x1, waiting for transfers between devices, shards(): lax.all_to_all(hit.reshape(devices, rows), ('dp', 'pp'), split_axis=0, co...  7.12 us
    psum x1, blocking collectives, shards(): lax.psum(lax.psum(view, axis_name='pp'), axis_name='dp')  5.98 us
    all_to_all x1, waiting for transfers between devices, shards(): lax.all_to_all(peak.reshape(devices, rows), ('dp', 'pp'), split_axis=0, c...  5.84 us
    all_to_all x1, waiting for transfers between devices, shards(): lax.all_to_all(mass.reshape(devices, rows), ('dp', 'pp'), split_axis=0, c...  5.78 us
  transfers between devices with their start and end apart: 4, of which 4 were waited for; matrix products, arithmetic and copies ran while one was open for 1% of the time, Pallas kernels for 0%

profile of v2, /device:TPU:0, one launch (start us, length us, event | category | flops | bytes accessed | tf_op | source)
XLA Modules:
  0.0 150.8 jit_solution(356328562407717495)
XLA Ops:
  7.2 0.0 copy-start.1
  7.2 0.0 all-gather.2.cloned.1.call-start
  7.2 0.7 all-gather.2.cloned.1.call-update
  7.9 0.9 dynamic-update-slice
  8.8 42.0 %all-reduce = s32[512]{0:T(512)S(1)} all-reduce(s32[512]{0:T(512)S(1)} %dynamic-update-slice), channel_id=1, replica_groups=mesh['dp'=4,'pp'=8] {'dp','pp'}, use_global_device_ids=true, to_apply=%add | all-reduce | flops 512 | bytes 4096
  50.8 24.9 %all-gather.2.cloned.1.call-done = bf16[512,4096]{1,0:T(8,128)(2,1)} async-done(((bf16[16,4096]{1,0:T(8,128)(2,1)}), bf16[512,4096]{1,0:T(8,128)(2,1)}) %all-gather.2.cloned.1.call-update) | async-done | bytes 4194320 | tf_op jit(solution)/shard_map/all_gather | solution.py:45
  75.7 0.0 copy-start
  75.7 3.2 %fusion = f32[512]{0:T(512)S(1)} fusion(bf16[512,4096]{1,0:T(8,128)(2,1)} %all-gather.2.cloned.1.call-done), kind=kLoop, calls=%fused_computation.2 | loop fusion | flops 6290944 | bytes 4196352 | tf_op jit(solution)/shard_map/reduce_sum | solution.py:10
  79.0 0.0 copy-done.1
  79.0 0.2 copy-done
  79.2 0.0 copy-start.2
  79.2 7.4 %fusion.8 = (f32[512]{0:T(512)S(1)}, f32[512,1024]{1,0:T(8,128)S(1)}) fusion(bf16[1024,4096]{1,0:T(8,128)(2,1)} %param.7, bf16[512,4096]{1,0:T(8,128)(2,1)S(1)} %copy-done, f32[4096]{0:T(1024)S(1)} %copy-done.1, f32[512]{0:T(512)S(1)} %add_rsqrt_fusion), kind=kOutput, calls=%fused_computation.17 | convolution fusion | flops 4303879680 | bytes 14700544 | tf_op jit(solution)/shard_map/while/body/eval_jaxpr/dot_general | solution.py:21
  86.6 0.7 all_to_all.22
  87.3 3.4 %all-to-all-start = ((f32[32,1,16]{2,1,0:T(1,128)}), f32[32,1,16]{2,1,0:T(1,128)S(1)}, u32[]{:S(2)}, u32[]{:S(2)}) async-start(f32[32,1,16]{2,1,0:T(1,128)} %bitcast), calls=%async_computation | async-start | bytes 32768 | tf_op jit(solution)/shard_map/all_to_all | solution.py:51
  90.7 0.6 exponential_reduce_fusion
  91.3 0.7 all_to_all.24
  92.0 5.8 %all-to-all-done = f32[32,1,16]{2,1,0:T(1,128)S(1)} async-done(((f32[32,1,16]{2,1,0:T(1,128)}), f32[32,1,16]{2,1,0:T(1,128)S(1)}, u32[]{:S(2)}, u32[]{:S(2)}) %all-to-all-start) | async-done | bytes 2080 | tf_op jit(solution)/shard_map/all_to_all | solution.py:51
  97.9 2.6 %all-to-all-start.1 = ((f32[32,1,16]{2,1,0:T(1,128)}), f32[32,1,16]{2,1,0:T(1,128)S(1)}, u32[]{:S(2)}, u32[]{:S(2)}) async-start(f32[32,1,16]{2,1,0:T(1,128)} %bitcast.1), calls=%async_computation.1 | async-start | bytes 32768 | tf_op jit(solution)/shard_map/all_to_all | solution.py:54
  100.4 0.0 copy-done.2
  100.4 0.6 dynamic_slice.9
  101.1 0.7 all_to_all.28
  101.7 0.1 reduce_max.20
  101.8 5.8 %all-to-all-done.1 = f32[32,1,16]{2,1,0:T(1,128)S(1)} async-done(((f32[32,1,16]{2,1,0:T(1,128)}), f32[32,1,16]{2,1,0:T(1,128)S(1)}, u32[]{:S(2)}, u32[]{:S(2)}) %all-to-all-start.1) | async-done | bytes 2080 | tf_op jit(solution)/shard_map/all_to_all | solution.py:54
  107.6 2.5 %all-to-all-start.2 = ((f32[32,1,16]{2,1,0:T(1,128)}), f32[32,1,16]{2,1,0:T(1,128)S(1)}, u32[]{:S(2)}, u32[]{:S(2)}) async-start(f32[32,1,16]{2,1,0:T(1,128)} %bitcast.4), calls=%async_computation.2 | async-start | bytes 32768 | tf_op jit(solution)/shard_map/all_to_all | solution.py:57
  110.1 7.1 %all-to-all-done.2 = f32[32,1,16]{2,1,0:T(1,128)S(1)} async-done(((f32[32,1,16]{2,1,0:T(1,128)}), f32[32,1,16]{2,1,0:T(1,128)S(1)}, u32[]{:S(2)}, u32[]{:S(2)}) %all-to-all-start.2) | async-done | bytes 2080 | tf_op jit(solution)/shard_map/all_to_all | solution.py:57
  117.2 0.1 reduce_sum.60
  117.3 1.1 fusion.7
  118.4 1.3 compare_select_fusion
  119.7 17.7 %psum.14 = f32[4]{0:T(128)S(1)} all-reduce(f32[4]{0:T(128)S(1)} %compare_select_fusion), channel_id=1, replica_groups=mesh['dp'=4,'pp'=8] {'pp'}, use_global_device_ids=true, to_apply=%region_8.9 | all-reduce | flops 4 | bytes 32 | tf_op jit(solution)/shard_map/psum | solution.py:67
  137.4 6.0 %psum.15 = f32[4]{0:T(128)S(1)} all-reduce(f32[4]{0:T(128)S(1)} %psum.14), channel_id=1, replica_groups=mesh['dp'=4,'pp'=8] {'dp'}, use_global_device_ids=true, to_apply=%region_9.10 | all-reduce | flops 4 | bytes 32 | tf_op jit(solution)/shard_map/psum | solution.py:67
  143.4 0.5 broadcast_multiply_fusion
  (4 shorter events, 0.0 us)
Async XLA Ops:
  7.2 71.8 %copy-start.1 = (f32[4096]{0:T(1024)S(1)}, f32[4096]{0:T(1024)}, u32[]{:S(2)}) copy-start(f32[4096]{0:T(1024)} %param.6) | copy-start | bytes 49156
  7.2 68.6 %all-gather.2.cloned.1.call-start = ((), (), s32[]{:S(2)}) async-start(), calls=%async_computation.3 | async-start | bytes 4325376 | tf_op jit(solution)/shard_map/all_gather | solution.py:45
  75.7 3.4 %copy-start = (bf16[512,4096]{1,0:T(8,128)(2,1)S(1)}, bf16[512,4096]{1,0:T(8,128)(2,1)}, u32[]{:S(2)}) copy-start(bf16[512,4096]{1,0:T(8,128)(2,1)} %all-gather.2.cloned.1.call-done) | copy-start | bytes 12582916
  79.2 21.2 %copy-start.2 = (s32[32]{0:T(128)S(1)}, s32[32]{0:T(128)}, u32[]{:S(2)}) copy-start(s32[32]{0:T(128)} %param.9) | copy-start | bytes 388
  87.3 10.5 %all-to-all-start = ((f32[32,1,16]{2,1,0:T(1,128)}), f32[32,1,16]{2,1,0:T(1,128)S(1)}, u32[]{:S(2)}, u32[]{:S(2)}) async-start(f32[32,1,16]{2,1,0:T(1,128)} %bitcast), calls=%async_computation | async-start | bytes 32768 | tf_op jit(solution)/shard_map/all_to_all | solution.py:51
  97.9 9.7 %all-to-all-start.1 = ((f32[32,1,16]{2,1,0:T(1,128)}), f32[32,1,16]{2,1,0:T(1,128)S(1)}, u32[]{:S(2)}, u32[]{:S(2)}) async-start(f32[32,1,16]{2,1,0:T(1,128)} %bitcast.1), calls=%async_computation.1 | async-start | bytes 32768 | tf_op jit(solution)/shard_map/all_to_all | solution.py:54
  107.6 9.6 %all-to-all-start.2 = ((f32[32,1,16]{2,1,0:T(1,128)}), f32[32,1,16]{2,1,0:T(1,128)S(1)}, u32[]{:S(2)}, u32[]{:S(2)}) async-start(f32[32,1,16]{2,1,0:T(1,128)} %bitcast.4), calls=%async_computation.2 | async-start | bytes 32768 | tf_op jit(solution)/shard_map/all_to_all | solution.py:57
Sparse Core Ops, SparseCore 0:
  11.1 64.6 all-gather.1
